TPU v7x, 32 devices: a whole 2x2x4 slice. The times are simulated.
32 devices in a mesh: dp: 4 (over y, x), expert: 8 (over z, core).
Axes of the slice: x: 2, y: 2, z: 4, core: 2. Of those that a mesh axis runs over, the one named last changes fastest.
Arguments:
- acts: bfloat16 [8, 512, 2560], P('expert', 'dp'), may hold values from -6 to 6
- out_grads: bfloat16 [8, 512, 768], P('expert', 'dp'), may hold values from -2 to 2
- next_tokens: bfloat16 [8, 512, 2560], P('expert', 'dp'), may hold values from -6 to 6
- master: float32 [8, 2560, 768], P('expert', 'dp'), may hold values from -0.125 to 0.125
- first_moment: float32 [8, 2560, 768], P('expert', 'dp'), may hold values from -6 to 6
- second_moment: float32 [8, 2560, 768], P('expert', 'dp'), may hold values from 0.5 to 20
- counts: int32 [4, 160], P('dp'), may hold values from 32 to 128
- selected: int32 [8], replicated, may hold values from 0 to 159
- old_place: int32 [8], replicated, may hold values from 0 to 7, each once
- new_place: int32 [8], replicated, may hold values from 0 to 7, each once
Outputs:
- new_master: float32 [8, 2560, 768], P('expert', 'dp')
- new_first: float32 [8, 2560, 768], P('expert', 'dp')
- new_second: float32 [8, 2560, 768], P('expert', 'dp')
- forward: bfloat16 [8, 512, 768], P('expert', 'dp')
Inputs may be any that keep to these rules, and one draw needn't show every extreme that they name: `old_place`: each holder index appears once. `new_place`: each holder index appears once.
All inputs are finite; a program needn't handle non-finite values.
Results may differ from a plain program's by a relative error of at most 0.012.
Values may be sent and summed in bfloat16 or wider, within the bound.
No kernel may reach another device: no remote copies, remote signals or barrier semaphores. Data moves between devices by JAX's collectives and lax.ppermute only.
A program may use at most 64 MiB of HBM per device.

v0:
```python
import jax
import jax.numpy as jnp
from jax import lax
from jax.sharding import PartitionSpec as P

beta_first = 0.9
beta_second = 0.95
bias_first = 1.0 - 0.9**10
bias_second = 1.0 - 0.95**10
learn_rate = 0.01
decay_rate = 0.1
epsilon = 1e-08


def adamw(weights, moment_one, moment_two, gradient):
    moment_one = beta_first * moment_one + (1.0 - beta_first) * gradient
    moment_two = beta_second * moment_two + (1.0 - beta_second) * gradient * gradient
    update = (
        moment_one / bias_first / (jnp.sqrt(moment_two / bias_second) + epsilon)
        + decay_rate * weights
    )
    return (weights - learn_rate * update, moment_one, moment_two)


def relocate_states(weights, moment_one, moment_two, order):
    holders = lax.axis_size("expert")
    shard_rows, width = weights.shape
    first = weights.reshape(holders, shard_rows // holders, width)
    second = moment_one.reshape(holders, shard_rows // holders, width)
    third = moment_two.reshape(holders, shard_rows // holders, width)
    relayed = (
        lax.all_to_all(
            first.astype(jnp.bfloat16), "expert", split_axis=0, concat_axis=0, tiled=True
        ).astype(first.dtype),
        lax.all_to_all(
            second.astype(jnp.bfloat16), "expert", split_axis=0, concat_axis=0, tiled=True
        ).astype(second.dtype),
        lax.all_to_all(
            third.astype(jnp.bfloat16), "expert", split_axis=0, concat_axis=0, tiled=True
        ).astype(third.dtype),
    )
    arranged = tuple((jnp.take(member, order, axis=0) for member in relayed))
    arrived = (
        lax.all_to_all(
            arranged[0].astype(jnp.bfloat16), "expert", split_axis=0, concat_axis=0, tiled=True
        ).astype(jnp.float32),
        lax.all_to_all(
            arranged[1].astype(jnp.bfloat16), "expert", split_axis=0, concat_axis=0, tiled=True
        ).astype(jnp.float32),
        lax.all_to_all(
            arranged[2].astype(jnp.bfloat16), "expert", split_axis=0, concat_axis=0, tiled=True
        ).astype(jnp.float32),
    )
    return tuple((member.reshape(shard_rows, width) for member in arrived))


def body(
    acts,
    out_grads,
    next_tokens,
    master,
    first_moment,
    second_moment,
    counts,
    selected,
    old_place,
    new_place,
):
    holders = lax.axis_size("expert")
    my_holder = lax.axis_index("expert")
    tokens_here = acts[0]
    grads_here = out_grads[0]
    shard_rows = master.shape[1]
    width = master.shape[2]
    positions = jnp.arange(holders, dtype=jnp.int32)
    expert_id = jnp.sum(jnp.where(old_place == my_holder, selected, 0))
    table = jnp.arange(counts.shape[1], dtype=jnp.int32)
    routed = jnp.sum(jnp.where(table == expert_id, counts[0], 0))
    live = jnp.arange(tokens_here.shape[0], dtype=jnp.int32) < routed
    masked = jnp.where(live[:, None], grads_here, jnp.zeros_like(grads_here))
    destination = jnp.sum(
        jnp.where(old_place[None, :] == positions[:, None], new_place[None, :], 0), axis=1
    )
    order = jnp.sum(
        jnp.where(destination[None, :] == positions[:, None], positions[None, :], 0), axis=1
    )
    groups = lax.axis_size("dp")
    rows_each = tokens_here.shape[0]
    columns = lax.all_to_all(tokens_here, "dp", split_axis=1, concat_axis=0, tiled=True)
    every = lax.all_gather(masked, "dp", axis=0, tiled=True)
    blocks = jnp.einsum(
        "stk,stf->skf",
        columns.reshape(groups, rows_each, shard_rows),
        every.reshape(groups, rows_each, width),
        preferred_element_type=jnp.float32,
    )
    rounded = lax.optimization_barrier(blocks.astype(jnp.bfloat16))
    gradient = jnp.sum(rounded.astype(jnp.float32), axis=0)
    updated = adamw(master[0], first_moment[0], second_moment[0], gradient)
    weights, moment_one, moment_two = relocate_states(updated[0], updated[1], updated[2], order)
    lowered = weights.astype(jnp.bfloat16)
    incoming = next_tokens[0]
    columns = incoming
    forward = jnp.dot(
        columns,
        lax.all_gather(lowered, "dp", axis=0, tiled=True),
        preferred_element_type=jnp.float32,
    )
    return (weights[None], moment_one[None], moment_two[None], forward.astype(jnp.bfloat16)[None])


def solution(mesh):
    return jax.shard_map(
        body,
        mesh=mesh,
        in_specs=(
            P("expert", "dp", None),
            P("expert", "dp", None),
            P("expert", "dp", None),
            P("expert", "dp", None),
            P("expert", "dp", None),
            P("expert", "dp", None),
            P("dp", None),
            P(),
            P(),
            P(),
        ),
        out_specs=(
            P("expert", "dp", None),
            P("expert", "dp", None),
            P("expert", "dp", None),
            P("expert", "dp", None),
        ),
        check_vma=False,
    )
```

profile of v0, /device:TPU:0, one launch (start us, length us, event | category | flops | bytes accessed | tf_op | source)
XLA Modules:
  0.0 236.5 jit_solution(4499890439265075193)
XLA Ops:
  7.2 1.5 copy.35
  8.7 1.1 copy.36
  9.8 5.2 %all-to-all-start = ((bf16[128,4,640]{2,0,1:T(8,128)(2,1)}), bf16[128,4,640]{2,0,1:T(8,128)(2,1)}, u32[]{:S(2)}, u32[]{:S(2)}) async-start(bf16[128,4,640]{2,0,1:T(8,128)(2,1)} %copy.36), calls=%async_computation | async-start | bytes 1310720 | tf_op jit(solution)/shard_map/all_to_all | solution.py:89
  15.0 0.6 fusion.7
  15.6 1.3 fusion.6
  16.9 0.6 iota_compare_fusion.2
  17.6 1.9 broadcast_multiply_fusion.1
  19.5 14.0 %all_gather.6 = bf16[512,768]{1,0:T(8,128)(2,1)S(1)} all-gather(bf16[128,768]{1,0:T(8,128)(2,1)S(1)} %bitcast_select_fusion), channel_id=1, replica_groups=mesh['dp'=4,'expert'=8] {'dp'}, dimensions={0}, use_global_device_ids=true | all-gather | bytes 983040 | tf_op jit(solution)/shard_map/all_gather | solution.py:90
  33.5 1.5 broadcast_multiply_fusion
  35.0 2.3 convert_bitcast_fusion
  37.3 1.9 convert_reduce_fusion
  39.2 2.8 %copy.38 = f32[640,768]{1,0:T(8,128)} copy(f32[640,768]{0,1:T(8,128)} %convert_reduce_fusion) | data formatting | bytes 3932160 | tf_op jit(solution)/shard_map/reduce_sum | solution.py:98
  42.0 5.2 %fusion.5 = (bf16[8,80,768]{2,1,0:T(8,128)(2,1)}, bf16[8,80,768]{2,1,0:T(8,128)(2,1)S(1)}, bf16[8,80,768]{2,1,0:T(8,128)(2,1)S(1)}) fusion(f32[8,80,768]{2,1,0:T(8,128)} %bitcast.39, f32[8,80,768]{2,1,0:T(8,128)} %bitcast.40, f32[8,80,768]{2,1,0:T(8,128)} %bitcast.45, f32[8,80,768]{2,1,0:T(8,128)S(1)} %bitcast.38), kind=kLoop, calls=%fused_computation.22 | loop fusion | flops 7864320 | bytes 10813440 | tf_op jit(solution)/shard_map/convert_element_type | solution.py:39
  47.3 29.7 %all_to_all.46 = bf16[8,80,768]{2,1,0:T(8,128)(2,1)S(1)} all-to-all(bf16[8,80,768]{2,1,0:T(8,128)(2,1)S(1)} %get-tuple-element.26), channel_id=1, replica_groups=mesh['dp'=4,'expert'=8] {'expert'}, dimensions={0} | all-to-all | bytes 1966080 | tf_op jit(solution)/shard_map/all_to_all | solution.py:32
  77.0 28.4 %all_to_all.47 = bf16[8,80,768]{2,1,0:T(8,128)(2,1)} all-to-all(bf16[8,80,768]{2,1,0:T(8,128)(2,1)S(1)} %get-tuple-element.27), channel_id=1, replica_groups=mesh['dp'=4,'expert'=8] {'expert'}, dimensions={0} | all-to-all | bytes 1966080 | tf_op jit(solution)/shard_map/all_to_all | solution.py:35
  105.4 3.6 %all-to-all-start.5 = ((bf16[8,80,768]{2,1,0:T(8,128)(2,1)}), bf16[8,80,768]{2,1,0:T(8,128)(2,1)S(1)}, u32[]{:S(2)}, u32[]{:S(2)}) async-start(bf16[8,80,768]{2,1,0:T(8,128)(2,1)} %get-tuple-element.25), calls=%async_computation.5 | async-start | bytes 1966080 | tf_op jit(solution)/shard_map/all_to_all | solution.py:38
  109.0 0.1 select_reduce_fusion.1
  109.1 0.1 select_reduce_fusion
  109.3 1.6 gather_fusion
  110.9 2.8 %gather_fusion.1 = bf16[8,80,768]{2,1,0:T(8,128)(2,1)} fusion(bf16[8,80,768]{2,1,0:T(8,128)(2,1)} %all_to_all.47, s32[1024]{0:T(1024)S(1)} %pad_clamp_fusion), kind=kCustom, calls=%fused_computation.1.clone | custom fusion | bytes 1966112 | tf_op jit(solution)/shard_map/jit(_take)/gather | solution.py:42
  113.7 20.3 %all-to-all-done.5 = bf16[8,80,768]{2,1,0:T(8,128)(2,1)S(1)} async-done(((bf16[8,80,768]{2,1,0:T(8,128)(2,1)}), bf16[8,80,768]{2,1,0:T(8,128)(2,1)S(1)}, u32[]{:S(2)}, u32[]{:S(2)}) %all-to-all-start.5) | async-done | bytes 983072 | tf_op jit(solution)/shard_map/all_to_all | solution.py:38
  134.0 1.6 gather_fusion.2
  135.6 3.1 %select_convert_fusion = (bf16[8,80,768]{2,1,0:T(8,128)(2,1)S(1)}, bf16[8,80,768]{2,1,0:T(8,128)(2,1)}, bf16[8,80,768]{2,1,0:T(8,128)(2,1)S(1)}) fusion(bf16[8,80,768]{2,1,0:T(8,128)(2,1)} %gather_fusion.2, pred[8]{0:T(512)(128)(4,1)S(1)} %compare_and_fusion, bf16[8,80,768]{2,1,0:T(8,128)(2,1)} %gather_fusion.1, bf16[8,80,768]{2,1,0:T(8,128)(2,1)S(1)} %copy-done.2), kind=kLoop, calls=%fused_computation.7 | loop fusion | flops 1474560 | bytes 5898248 | tf_op jit(solution)/shard_map/convert_element_type | solution.py:51
  138.7 28.3 %all_to_all.48 = bf16[8,80,768]{2,1,0:T(8,128)(2,1)} all-to-all(bf16[8,80,768]{2,1,0:T(8,128)(2,1)S(1)} %get-tuple-element.30), channel_id=1, replica_groups=mesh['dp'=4,'expert'=8] {'expert'}, dimensions={0} | all-to-all | bytes 1966080 | tf_op jit(solution)/shard_map/all_to_all | solution.py:44
  167.0 28.4 %all_to_all.49 = bf16[8,80,768]{2,1,0:T(8,128)(2,1)} all-to-all(bf16[8,80,768]{2,1,0:T(8,128)(2,1)S(1)} %get-tuple-element.28), channel_id=1, replica_groups=mesh['dp'=4,'expert'=8] {'expert'}, dimensions={0} | all-to-all | bytes 1966080 | tf_op jit(solution)/shard_map/all_to_all | solution.py:50
  195.4 3.6 %all-to-all-start.4 = ((bf16[8,80,768]{2,1,0:T(8,128)(2,1)}), bf16[8,80,768]{2,1,0:T(8,128)(2,1)S(1)}, u32[]{:S(2)}, u32[]{:S(2)}) async-start(bf16[8,80,768]{2,1,0:T(8,128)(2,1)} %get-tuple-element.29), calls=%async_computation.4 | async-start | bytes 1966080 | tf_op jit(solution)/shard_map/all_to_all | solution.py:47
  199.0 1.4 bitcast_convert_fusion.2
  200.5 1.4 bitcast_convert_fusion
  201.9 22.2 %all-to-all-done.4 = bf16[8,80,768]{2,1,0:T(8,128)(2,1)S(1)} async-done(((bf16[8,80,768]{2,1,0:T(8,128)(2,1)}), bf16[8,80,768]{2,1,0:T(8,128)(2,1)S(1)}, u32[]{:S(2)}, u32[]{:S(2)}) %all-to-all-start.4) | async-done | bytes 983072 | tf_op jit(solution)/shard_map/all_to_all | solution.py:47
  224.1 1.4 bitcast_convert_fusion.1
  225.5 3.3 %fusion.1 = bf16[1,128,768]{1,2,0:T(8,128)(2,1)S(1)} fusion(bf16[2560,768]{1,0:T(8,128)(2,1)} %all-gather.2.cloned.1.call-done, bf16[1,128,2560]{2,1,0:T(8,128)(2,1)S(1)} %copy-done), kind=kOutput, calls=%fused_computation.13 | convolution fusion | flops 503414784 | bytes 4784128 | tf_op jit(solution)/shard_map/dot_general | solution.py:104
  228.8 0.8 copy.39
  (28 shorter events, 0.3 us)
Async XLA Ops:
  7.2 218.3 %copy-start = (bf16[1,128,2560]{2,1,0:T(8,128)(2,1)S(1)}, bf16[1,128,2560]{2,1,0:T(8,128)(2,1)}, u32[]{:S(2)}) copy-start(bf16[1,128,2560]{2,1,0:T(8,128)(2,1)} %param.14) | copy-start | bytes 1966084
  7.2 7.8 %copy-start.8 = (s32[8]{0:T(128)S(1)}, s32[8]{0:T(128)}, u32[]{:S(2)}) copy-start(s32[8]{0:T(128)} %param.20) | copy-start | bytes 100
  7.2 7.8 %copy-start.7 = (s32[8]{0:T(128)S(1)}, s32[8]{0:T(128)}, u32[]{:S(2)}) copy-start(s32[8]{0:T(128)} %param.19) | copy-start | bytes 100
  7.2 8.4 %copy-start.6 = (s32[1,160]{1,0:T(1,128)S(1)}, s32[1,160]{1,0:T(1,128)}, u32[]{:S(2)}) copy-start(s32[1,160]{1,0:T(1,128)} %param.18) | copy-start | bytes 1924
  9.8 25.2 %all-to-all-start = ((bf16[128,4,640]{2,0,1:T(8,128)(2,1)}), bf16[128,4,640]{2,0,1:T(8,128)(2,1)}, u32[]{:S(2)}, u32[]{:S(2)}) async-start(bf16[128,4,640]{2,0,1:T(8,128)(2,1)} %copy.36), calls=%async_computation | async-start | bytes 1310720 | tf_op jit(solution)/shard_map/all_to_all | solution.py:89
  17.5 1.9 copy-start.5
  17.6 16.0 %copy-start.4 = (f32[1,640,768]{2,1,0:T(8,128)S(1)}, f32[1,640,768]{2,1,0:T(8,128)}, u32[]{:S(2)}) copy-start(f32[1,640,768]{2,1,0:T(8,128)} %param.17) | copy-start | bytes 5898244
  77.0 32.0 %copy-start.9 = (s32[8]{0:T(128)S(1)}, s32[8]{0:T(128)}, u32[]{:S(2)}) copy-start(s32[8]{0:T(128)} %param.21) | copy-start | bytes 100
  105.4 28.6 %all-to-all-start.5 = ((bf16[8,80,768]{2,1,0:T(8,128)(2,1)}), bf16[8,80,768]{2,1,0:T(8,128)(2,1)S(1)}, u32[]{:S(2)}, u32[]{:S(2)}) async-start(bf16[8,80,768]{2,1,0:T(8,128)(2,1)} %get-tuple-element.25), calls=%async_computation.5 | async-start | bytes 1966080 | tf_op jit(solution)/shard_map/all_to_all | solution.py:38
  108.9 116.5 %all-gather.2.cloned.1.call-start = ((), (), s32[]{:S(2)}) async-start(), calls=%async_computation.7 | async-start | bytes 4915200 | tf_op jit(solution)/shard_map/all_gather | solution.py:106
  110.9 24.7 %copy-start.2 = (bf16[8,80,768]{2,1,0:T(8,128)(2,1)S(1)}, bf16[8,80,768]{2,1,0:T(8,128)(2,1)}, u32[]{:S(2)}) copy-start(bf16[8,80,768]{2,1,0:T(8,128)(2,1)} %gather_fusion) | copy-start | bytes 2949124
  167.0 32.0 %copy-start.1 = (bf16[8,80,768]{2,1,0:T(8,128)(2,1)S(1)}, bf16[8,80,768]{2,1,0:T(8,128)(2,1)}, u32[]{:S(2)}) copy-start(bf16[8,80,768]{2,1,0:T(8,128)(2,1)} %all_to_all.48) | copy-start | bytes 2949124
  195.4 28.6 %all-to-all-start.4 = ((bf16[8,80,768]{2,1,0:T(8,128)(2,1)}), bf16[8,80,768]{2,1,0:T(8,128)(2,1)S(1)}, u32[]{:S(2)}, u32[]{:S(2)}) async-start(bf16[8,80,768]{2,1,0:T(8,128)(2,1)} %get-tuple-element.29), calls=%async_computation.4 | async-start | bytes 1966080 | tf_op jit(solution)/shard_map/all_to_all | solution.py:47
  199.0 1.5 copy-start.3
Sparse Core Ops, SparseCore 0:
  167.1 48.3 all-gather.1
where the time goes:
time: 237 us
  blocking collectives  129 us (54%)
  waiting for transfers between devices  42.5 us (18%)
  other arithmetic  20.7 us (9%)
  between operations  14.2 us (6%)
  local copies, waits for them, and re-layouts  12.3 us (5%)
  starting transfers between devices  12.3 us (5%)
  matrix products  5.65 us (2%)
    all_to_all x1, blocking collectives, relocate_states(): lax.all_to_all(first.astype(jnp.bfloat16), 'expert', split_axis=0, concat...  29.7 us
    all_to_all x1, blocking collectives, relocate_states(): lax.all_to_all(arranged[2].astype(jnp.bfloat16), 'expert', split_axis=0,...  28.4 us
    all_to_all x1, blocking collectives, relocate_states(): lax.all_to_all(second.astype(jnp.bfloat16), 'expert', split_axis=0, conca...  28.4 us
    all_to_all x1, blocking collectives, relocate_states(): lax.all_to_all(arranged[0].astype(jnp.bfloat16), 'expert', split_axis=0,...  28.3 us
    all_to_all x1, waiting for transfers between devices, relocate_states(): lax.all_to_all(arranged[1].astype(jnp.bfloat16), 'expert', split_axis=0,...  22.2 us
    all_to_all x1, waiting for transfers between devices, relocate_states(): lax.all_to_all(third.astype(jnp.bfloat16), 'expert', split_axis=0, concat...  20.3 us
    all_gather x1, blocking collectives, body(): every = lax.all_gather(masked, 'dp', axis=0, tiled=True)  14 us
    gather x3, local copies, waits for them, and re-layouts, relocate_states(): arranged = tuple((jnp.take(member, order, axis=0) for member in relayed))  6.02 us
  transfers between devices with their start and end apart: 4, of which 2 were waited for; matrix products, arithmetic and copies ran while one was open for 6% of the time, Pallas kernels for 0%

commit v1 on v0

--- a/solution.py
+++ b/solution.py
@@ -1,3 +1,6 @@
+import itertools
+import math
+
 import jax
 import jax.numpy as jnp
 from jax import lax
@@ -11,6 +14,9 @@
 decay_rate = 0.1
 epsilon = 1e-08
 
+CORES = 2
+ROUTE_LIMIT = 24
+
 
 def adamw(weights, moment_one, moment_two, gradient):
     moment_one = beta_first * moment_one + (1.0 - beta_first) * gradient
@@ -20,6 +26,184 @@
         + decay_rate * weights
     )
     return (weights - learn_rate * update, moment_one, moment_two)
+
+
+def pick(table, index):
+    slots = jnp.arange(table.shape[0], dtype=jnp.int32)
+    return jnp.sum(jnp.where(index[..., None] == slots, table, 0), axis=-1)
+
+
+def some_colouring(destination, source, holders):
+    every = jnp.arange(holders, dtype=jnp.int32)
+    beside = every ^ 1
+    hop = pick(source, pick(destination, beside) ^ 1)
+    least = every
+    for _ in range(holders // CORES - 1):
+        least = jnp.minimum(every, pick(least, hop))
+    return (least > pick(least, beside)).astype(jnp.int32)
+
+
+def rank_of(perm):
+    size = perm.shape[0]
+    slots = jnp.arange(size, dtype=jnp.int32)
+    smaller = jnp.sum(
+        jnp.where(
+            (perm[None, :] < perm[:, None]) & (slots[None, :] > slots[:, None]), 1, 0
+        ),
+        axis=1,
+    )
+    weight = jnp.array([math.factorial(size - 1 - i) for i in range(size)], jnp.int32)
+    return jnp.sum(smaller * weight)
+
+
+def busiest(perm):
+    return max(
+        max(
+            sum(src <= cut < dst for src, dst in enumerate(perm)),
+            sum(dst <= cut < src for src, dst in enumerate(perm)),
+        )
+        for cut in range(len(perm))
+    )
+
+
+def best_pairs(chips):
+    orders = list(itertools.permutations(range(chips)))
+    best = {}
+    codes = []
+    for one, two in itertools.product(orders, repeat=CORES):
+        traffic = tuple(tuple(sorted(ends)) for ends in zip(one, two))
+        codes.append(traffic)
+        cost = busiest(one) + busiest(two)
+        code = orders.index(one) * len(orders) + orders.index(two)
+        best[traffic] = min(best.get(traffic, (cost, code)), (cost, code))
+    return orders, [best[traffic][1] for traffic in codes]
+
+
+def direct_body(
+    acts,
+    out_grads,
+    next_tokens,
+    master,
+    first_moment,
+    second_moment,
+    counts,
+    selected,
+    old_place,
+    new_place,
+):
+    holders = lax.axis_size("expert")
+    groups = lax.axis_size("dp")
+    me = lax.axis_index("expert")
+    chips = holders // CORES
+    beside = [(i, i ^ 1) for i in range(holders)]
+    tokens_here = acts[0]
+    grads_here = out_grads[0]
+    rows_each = tokens_here.shape[0]
+    shard_rows, width = master.shape[1:]
+    half = shard_rows // CORES
+    positions = jnp.arange(holders, dtype=jnp.int32)
+    expert_id = jnp.sum(jnp.where(old_place == me, selected, 0))
+    table = jnp.arange(counts.shape[1], dtype=jnp.int32)
+    routed = jnp.sum(jnp.where(table == expert_id, counts[0], 0))
+    live = jnp.arange(rows_each, dtype=jnp.int32) < routed
+    masked = jnp.where(live[:, None], grads_here, jnp.zeros_like(grads_here))
+
+    packed = jnp.concatenate(
+        [
+            tokens_here.reshape(rows_each, groups, shard_rows).transpose(1, 0, 2),
+            jnp.broadcast_to(masked, (groups, rows_each, width)),
+        ],
+        axis=2,
+    )
+    packed = lax.all_to_all(packed, "dp", split_axis=0, concat_axis=0, tiled=True)
+    next_columns = lax.all_to_all(
+        next_tokens[0].reshape(rows_each, groups, shard_rows).transpose(1, 0, 2),
+        "dp",
+        split_axis=0,
+        concat_axis=0,
+        tiled=True,
+    )
+
+    destination = jnp.sum(
+        jnp.where(old_place[None, :] == positions[:, None], new_place[None, :], 0), axis=1
+    )
+    source = jnp.sum(
+        jnp.where(new_place[None, :] == positions[:, None], old_place[None, :], 0), axis=1
+    )
+    orders, best = best_pairs(chips)
+    chip_slots = jnp.arange(chips, dtype=jnp.int32)
+    edge = CORES * chip_slots
+    edge = edge + pick(some_colouring(destination, source, holders), edge)
+    code = rank_of(pick(destination, edge) // CORES) * len(orders) + rank_of(
+        pick(destination, edge ^ 1) // CORES
+    )
+    code = pick(jnp.array(best, jnp.int32), code[None])[0]
+    route_one = code // len(orders)
+    route_two = code % len(orders)
+    flat_orders = jnp.array(orders, jnp.int32).reshape(-1)
+    to_one = pick(flat_orders, route_one * chips + chip_slots)
+    rider = CORES * chip_slots + (
+        pick(destination, CORES * chip_slots) // CORES != to_one
+    ).astype(jnp.int32)
+    chip = me // CORES
+    core = me % CORES
+    sends_one = pick(rider, chip[None])[0] == me
+    gets_one = jnp.sum(jnp.where(pick(destination, rider) == me, 1, 0)) > 0
+
+    gradient = jnp.einsum(
+        "stk,stf->kf",
+        packed[:, :, :shard_rows],
+        packed[:, :, shard_rows:],
+        preferred_element_type=jnp.float32,
+    )
+    states = adamw(master[0], first_moment[0], second_moment[0], gradient)
+    states = jnp.stack([member.astype(jnp.bfloat16) for member in states])
+    keep = lax.dynamic_slice_in_dim(states, core * half, half, axis=1)
+    give = lax.dynamic_slice_in_dim(states, (1 - core) * half, half, axis=1)
+    take = lax.ppermute(give, "expert", beside)
+    one = jnp.where(sends_one, keep, take)
+    two = jnp.where(sends_one, take, keep)
+
+    def pairs(order):
+        return [
+            (z * CORES + c, order[z] * CORES + c)
+            for z in range(chips)
+            for c in range(CORES)
+        ]
+
+    def leg(order):
+        return lambda value: lax.ppermute(value, "expert", pairs(order))
+
+    one, two, route_one, route_two = lax.optimization_barrier(
+        (one, two, route_one, route_two)
+    )
+    one = lax.switch(route_one, [leg(order) for order in orders], one)
+    one, two = lax.optimization_barrier((one, two))
+    two = lax.switch(route_two, [leg(order) for order in orders], two)
+    one, two = lax.optimization_barrier((one, two))
+
+    def join(index):
+        mine = jnp.where(gets_one, one[index], two[index])
+        other = jnp.where(gets_one, two[index], one[index])
+        other = lax.ppermute(other, "expert", beside)
+        return jnp.where(
+            core == 0,
+            jnp.concatenate([mine, other], axis=0),
+            jnp.concatenate([other, mine], axis=0),
+        )
+
+    arrived = [join(index) for index in range(3)]
+    partial = jnp.einsum(
+        "stk,kf->stf", next_columns, arrived[0], preferred_element_type=jnp.float32
+    ).astype(jnp.bfloat16)
+    partial = lax.all_to_all(partial, "dp", split_axis=0, concat_axis=0, tiled=True)
+    forward = jnp.sum(partial.astype(jnp.float32), axis=0)
+    return (
+        arrived[0].astype(jnp.float32)[None],
+        arrived[1].astype(jnp.float32)[None],
+        arrived[2].astype(jnp.float32)[None],
+        forward.astype(jnp.bfloat16)[None],
+    )
 
 
 def relocate_states(weights, moment_one, moment_two, order):
@@ -54,7 +238,7 @@
     return tuple((member.reshape(shard_rows, width) for member in arrived))
 
 
-def body(
+def relay_body(
     acts,
     out_grads,
     next_tokens,
@@ -110,8 +294,10 @@
 
 
 def solution(mesh):
+    chips = mesh.shape["expert"] // CORES
+    few = mesh.shape["expert"] % CORES == 0 and math.factorial(chips) <= ROUTE_LIMIT
     return jax.shard_map(
-        body,
+        direct_body if few else relay_body,
         mesh=mesh,
         in_specs=(
             P("expert", "dp", None),

time: 237 us -> 150 us (0.63)
  the two profiles are of different devices: /device:TPU:0 before, /device:TPU:8 now
where the time goes in v1:
time: 150 us
  waiting for transfers between devices  88.7 us (59%)
  other arithmetic  22.7 us (15%)
  starting transfers between devices  19.7 us (13%)
  matrix products  7.61 us (5%)
  between operations  5.43 us (4%)
  local copies, waits for them, and re-layouts  5.32 us (4%)
    ppermute x2, waiting for transfers between devices, leg(): return lambda value: lax.ppermute(value, 'expert', pairs(order))  66.8 us
    all_to_all x1, waiting for transfers between devices, direct_body(): lax.all_to_all(packed, 'dp', split_axis=0, concat_axis=0, tiled=True)  15 us
    ppermute x2, starting transfers between devices, leg(): return lambda value: lax.ppermute(value, 'expert', pairs(order))  7.05 us
    all_to_all x1, waiting for transfers between devices, direct_body(): lax.all_to_all(partial, 'dp', split_axis=0, concat_axis=0, tiled=True)  5.6 us
    dot_general x1, matrix products, direct_body(): jnp.einsum('stk,stf->kf', packed[:, :, :shard_rows], packed[:, :, shard_r...  4.8 us
    all_to_all x1, starting transfers between devices, direct_body(): lax.all_to_all(next_tokens[0].reshape(rows_each, groups, shard_rows).tran...  4.17 us
    all_to_all x1, starting transfers between devices, direct_body(): lax.all_to_all(partial, 'dp', split_axis=0, concat_axis=0, tiled=True)  4.14 us
    all_to_all x1, starting transfers between devices, direct_body(): lax.all_to_all(packed, 'dp', split_axis=0, concat_axis=0, tiled=True)  3.85 us
  transfers between devices with their start and end apart: 9, of which 5 were waited for; matrix products, arithmetic and copies ran while one was open for 18% of the time, Pallas kernels for 0%

profile of v1, /device:TPU:8, one launch (start us, length us, event | category | flops | bytes accessed | tf_op | source)
XLA Modules:
  0.0 149.5 jit_solution(15445322855619014789)
XLA Ops:
  0.6 1.3 fusion.27
  2.0 2.0 %fusion.23 = s32[]{:T(128)} fusion(s32[160]{0:T(256)} %bitcast.75, s32[]{:T(128)} %fusion.27), kind=kLoop, calls=%fused_computation.91 | loop fusion | flops 479 | bytes 648 | tf_op jit(solution)/shard_map/reduce_sum | solution.py:107
  4.0 0.6 iota_compare_fusion.12
  4.6 1.4 copy.33
  6.5 1.2 pad_maximum_fusion.1
  7.8 3.8 %all-to-all-start = ((bf16[4,128,1408]{2,1,0:T(8,128)(2,1)}), bf16[4,128,1408]{2,1,0:T(8,128)(2,1)S(1)}, u32[]{:S(2)}, u32[]{:S(2)}) async-start(bf16[4,128,1408]{2,1,0:T(8,128)(2,1)} %pad_maximum_fusion.1), calls=%async_computation | async-start | bytes 2883584 | tf_op jit(solution)/shard_map/all_to_all | solution.py:118
  12.9 1.1 copy.37
  14.6 15.0 %all-to-all-done = bf16[4,128,1408]{2,1,0:T(8,128)(2,1)S(1)} async-done(((bf16[4,128,1408]{2,1,0:T(8,128)(2,1)}), bf16[4,128,1408]{2,1,0:T(8,128)(2,1)S(1)}, u32[]{:S(2)}, u32[]{:S(2)}) %all-to-all-start) | async-done | bytes 1441824 | tf_op jit(solution)/shard_map/all_to_all | solution.py:118
  29.6 4.2 %all-to-all-start.1 = ((bf16[4,128,640]{2,1,0:T(8,128)(2,1)}), bf16[4,128,640]{2,1,0:T(8,128)(2,1)}, u32[]{:S(2)}, u32[]{:S(2)}) async-start(bf16[4,128,640]{2,1,0:T(8,128)(2,1)} %bitcast.20), calls=%async_computation.1 | async-start | bytes 1310720 | tf_op jit(solution)/shard_map/all_to_all | solution.py:119
  33.7 4.8 %fusion.17 = (bf16[1,640,768]{2,1,0:T(8,128)(2,1)S(1)}, bf16[1,640,768]{2,1,0:T(8,128)(2,1)S(1)}, bf16[1,640,768]{2,1,0:T(8,128)(2,1)S(1)}) fusion(f32[1,640,768]{2,1,0:T(8,128)} %param.65, f32[1,640,768]{2,1,0:T(8,128)} %param.66, f32[1,640,768]{2,1,0:T(8,128)} %param.67, bf16[4,128,1408]{2,1,0:T(8,128)(2,1)S(1)} %all-to-all-done), kind=kOutput, calls=%fused_computation.31 | convolution fusion | flops 512163840 | bytes 10289152 | tf_op jit(solution)/shard_map/stk,stf->kf/dot_general | solution.py:153
  38.9 1.2 constant_dynamic-slice_fusion
  40.7 0.6 multiply_reduce_fusion
  42.7 0.6 select_reduce_fusion
  45.5 0.6 fusion.26
  47.0 0.6 fusion.25
  48.3 3.5 %broadcast_select_fusion = (bf16[3,320,768]{2,1,0:T(8,128)(2,1)}, bf16[3,320,768]{2,1,0:T(8,128)(2,1)}) fusion(bf16[3,320,768]{2,1,0:T(8,128)(2,1)} %collective-permute-done.48, pred[]{:T(512)S(6)} %eq.253, bf16[3,640,768]{2,1,0:T(8,128)(2,1)S(1)} %pad_maximum_fusion, s32[]{:T(128)S(6)} %select_n.265), kind=kLoop, calls=%fused_computation.10 | loop fusion | flops 1474560 | bytes 5898245 | tf_op jit(solution)/shard_map/jit(_where)/select_n | solution.py:165
  51.8 37.8 %conditional.2 = (bf16[3,320,768]{2,1,0:T(8,128)(2,1)}) conditional(s32[]{:T(128)} %clamp.6, bf16[3,320,768]{2,1,0:T(8,128)(2,1)} %get-tuple-element.111, bf16[3,320,768]{2,1,0:T(8,128)(2,1)} %get-tuple-element.111, bf16[3,320,768]{2,1,0:T(8,128)(2,1)} %get-tuple-element.111, ...), branch_computations={%region_23.24_spmd, %region_24.25_spmd, %region_25.26_spmd, %regio... | conditional | bytes 5898288 | solution.py:180
  51.8 3.5 %collective-permute-start.3 = (bf16[3,320,768]{2,1,0:T(8,128)(2,1)}, bf16[3,320,768]{2,1,0:T(8,128)(2,1)}, u32[]{:S(2)}, u32[]{:S(2)}) collective-permute-start(bf16[3,320,768]{2,1,0:T(8,128)(2,1)} %param.3), channel_id=1, source_target_pairs={{0,0},{1,1},{2,4},{3,5},{4,6},{5,7},{6,2},{7,3},{8,8},{9,9},{10,12... | collective-permute-start | bytes 4423688 | tf_op jit(solution)/shard_map/cond/branch_3_fun/ppermute | solution.py:175
  55.3 34.3 %collective-permute-done.3 = bf16[3,320,768]{2,1,0:T(8,128)(2,1)} collective-permute-done((bf16[3,320,768]{2,1,0:T(8,128)(2,1)}, bf16[3,320,768]{2,1,0:T(8,128)(2,1)}, u32[]{:S(2)}, u32[]{:S(2)}) %collective-permute-start.3) | collective-permute-done | bytes 1474592 | tf_op jit(solution)/shard_map/cond/branch_3_fun/ppermute | solution.py:175
  89.6 36.0 %conditional.3 = (bf16[3,320,768]{2,1,0:T(8,128)(2,1)}) conditional(s32[]{:T(128)} %clamp.7, bf16[3,320,768]{2,1,0:T(8,128)(2,1)} %get-tuple-element.115, bf16[3,320,768]{2,1,0:T(8,128)(2,1)} %get-tuple-element.115, bf16[3,320,768]{2,1,0:T(8,128)(2,1)} %get-tuple-element.115, ...), branch_computations={%region_47.48_spmd, %region_48.49_spmd, %region_49.50_spmd, %regio... | conditional | bytes 5898288 | solution.py:182
  89.6 3.6 %collective-permute-start.35 = (bf16[3,320,768]{2,1,0:T(8,128)(2,1)}, bf16[3,320,768]{2,1,0:T(8,128)(2,1)}, u32[]{:S(2)}, u32[]{:S(2)}) collective-permute-start(bf16[3,320,768]{2,1,0:T(8,128)(2,1)} %param.35), channel_id=1, source_target_pairs={{0,2},{1,3},{2,6},{3,7},{4,4},{5,5},{6,0},{7,1},{8,10},{9,11},{10,... | collective-permute-start | bytes 4423688 | tf_op jit(solution)/shard_map/cond/branch_11_fun/ppermute | solution.py:175
  93.2 32.5 %collective-permute-done.35 = bf16[3,320,768]{2,1,0:T(8,128)(2,1)} collective-permute-done((bf16[3,320,768]{2,1,0:T(8,128)(2,1)}, bf16[3,320,768]{2,1,0:T(8,128)(2,1)}, u32[]{:S(2)}, u32[]{:S(2)}) %collective-permute-start.35) | collective-permute-done | bytes 1474592 | tf_op jit(solution)/shard_map/cond/branch_11_fun/ppermute | solution.py:175
  125.7 2.9 %broadcast_select_fusion.2 = (bf16[1,320,768]{2,1,0:T(8,128)(2,1)S(1)}, bf16[320,768]{1,0:T(8,128)(2,1)S(1)}, bf16[1,320,768]{2,1,0:T(8,128)(2,1)S(1)}, bf16[320...) fusion(pred[]{:T(512)S(6)} %gt.36, bf16[3,320,768]{2,1,0:T(8,128)(2,1)} %get-tuple-element.152, ...), kind=kLoop, calls=%fused_computation.38 | loop fusion | flops 1474560 | bytes 5898241 | tf_op jit(solution)/shard_map/jit(_where)/select_n | solution.py:186
  128.6 0.5 collective-permute-start.51
  129.1 1.3 collective-permute-done.49
  130.4 2.8 %fusion.5 = bf16[4,128,768]{1,2,0:T(8,128)(2,1)} fusion(bf16[4,128,640]{2,1,0:T(8,128)(2,1)} %all-to-all-done.1, bf16[320,768]{1,0:T(8,128)(2,1)S(1)} %collective-permute-done.49, bf16[320,768]{1,0:T(8,128)(2,1)S(1)} %bitcast.71, pred[]{:T(512)S(6)} %eq.101), kind=kOutput, calls=%fused_computation.14 | convolution fusion | flops 508133376 | bytes 2424833 | tf_op jit(solution)/shard_map/stk,kf->stf/dot_general | solution.py:196
  133.2 4.1 %all-to-all-start.2 = ((bf16[4,128,768]{1,2,0:T(8,128)(2,1)}), bf16[4,128,768]{1,2,0:T(8,128)(2,1)S(1)}, u32[]{:S(2)}, u32[]{:S(2)}) async-start(bf16[4,128,768]{1,2,0:T(8,128)(2,1)} %fusion.5), calls=%async_computation.2 | async-start | bytes 1572864 | tf_op jit(solution)/shard_map/all_to_all | solution.py:199
  137.4 1.5 fusion.6
  138.8 2.6 %fusion.8 = f32[1,640,768]{2,1,0:T(8,128)} fusion(bf16[1,320,768]{2,1,0:T(8,128)(2,1)} %bitcast.16, bf16[1,320,768]{2,1,0:T(8,128)(2,1)S(1)} %get-tuple-element.141, pred[]{:T(512)S(6)} %eq.101), kind=kLoop, calls=%fused_computation.20 | loop fusion | flops 4915200 | bytes 2949121 | tf_op jit(solution)/shard_map/convert_element_type | solution.py:204
  141.5 1.5 fusion.7
  142.9 5.6 %all-to-all-done.2 = bf16[4,128,768]{1,2,0:T(8,128)(2,1)S(1)} async-done(((bf16[4,128,768]{1,2,0:T(8,128)(2,1)}), bf16[4,128,768]{1,2,0:T(8,128)(2,1)S(1)}, u32[]{:S(2)}, u32[]{:S(2)}) %all-to-all-start.2) | async-done | bytes 786464 | tf_op jit(solution)/shard_map/all_to_all | solution.py:199
  148.7 0.8 copy.39
  (50 shorter events, 3.8 us)
Async XLA Ops:
  0.6 5.7 %copy-start.1 = (bf16[1,128,768]{2,1,0:T(8,128)(2,1)S(1)}, bf16[1,128,768]{2,1,0:T(8,128)(2,1)}, u32[]{:S(2)}) copy-start(bf16[1,128,768]{2,1,0:T(8,128)(2,1)} %param.63) | copy-start | bytes 589828
  7.8 3.9 %copy-start.3 = (s32[8]{0:T(128)S(1)}, s32[8]{0:T(128)}, u32[]{:S(2)}) copy-start(s32[8]{0:T(128)} %param.70) | copy-start | bytes 100
  7.8 3.9 %copy-start.5 = (s32[8]{0:T(128)S(1)}, s32[8]{0:T(128)}, u32[]{:S(2)}) copy-start(s32[8]{0:T(128)} %param.71) | copy-start | bytes 100
  7.8 4.8 %copy-start = (bf16[1,128,2560]{2,1,0:T(8,128)(2,1)S(1)}, bf16[1,128,2560]{2,1,0:T(8,128)(2,1)}, u32[]{:S(2)}) copy-start(bf16[1,128,2560]{2,1,0:T(8,128)(2,1)} %param.64) | copy-start | bytes 1966084
  7.8 21.8 %all-to-all-start = ((bf16[4,128,1408]{2,1,0:T(8,128)(2,1)}), bf16[4,128,1408]{2,1,0:T(8,128)(2,1)S(1)}, u32[]{:S(2)}, u32[]{:S(2)}) async-start(bf16[4,128,1408]{2,1,0:T(8,128)(2,1)} %pad_maximum_fusion.1), calls=%async_computation | async-start | bytes 2883584 | tf_op jit(solution)/shard_map/all_to_all | solution.py:118
  29.6 99.5 %all-to-all-start.1 = ((bf16[4,128,640]{2,1,0:T(8,128)(2,1)}), bf16[4,128,640]{2,1,0:T(8,128)(2,1)}, u32[]{:S(2)}, u32[]{:S(2)}) async-start(bf16[4,128,640]{2,1,0:T(8,128)(2,1)} %bitcast.20), calls=%async_computation.1 | async-start | bytes 1310720 | tf_op jit(solution)/shard_map/all_to_all | solution.py:119
  38.9 1.9 %copy-start.4 = (s32[4]{0:T(128)S(1)}, s32[4]{0:T(128)}, u32[]{:S(2)}) copy-start(s32[4]{0:T(128)} %constant.103.clone) | copy-start | bytes 52
  38.9 3.8 %copy-start.2 = (s32[576]{0:T(1024)S(1)}, s32[576]{0:T(1024)}, u32[]{:S(2)}) copy-start(s32[576]{0:T(1024)} %constant.104.clone) | copy-start | bytes 6916
  38.9 6.4 %copy-start.6 = (s32[96]{0:T(128)S(1)}, s32[96]{0:T(128)}, u32[]{:S(2)}) copy-start(s32[96]{0:T(128)} %constant.113) | copy-start | bytes 1156
  40.1 8.2 %collective-permute-start.48 = (bf16[3,320,768]{2,1,0:T(8,128)(2,1)}, bf16[3,320,768]{2,1,0:T(8,128)(2,1)}, u32[]{:S(2)}, u32[]{:S(2)}) collective-permute-start(bf16[3,320,768]{2,1,0:T(8,128)(2,1)} %constant_dynamic-slice_fusion), channel_id=1, source_target_pairs={{0,1},{1,0},{2,3},{3,2},{4,5},{5,4},{6,7},{7,6},{8,9},{9,8},{10,11... | collective-permute-start | bytes 4423688 | tf_op jit(solution)/shard_map/ppermute | solution.py:163
  51.8 37.8 %collective-permute-start.3 = (bf16[3,320,768]{2,1,0:T(8,128)(2,1)}, bf16[3,320,768]{2,1,0:T(8,128)(2,1)}, u32[]{:S(2)}, u32[]{:S(2)}) collective-permute-start(bf16[3,320,768]{2,1,0:T(8,128)(2,1)} %param.3), channel_id=1, source_target_pairs={{0,0},{1,1},{2,4},{3,5},{4,6},{5,7},{6,2},{7,3},{8,8},{9,9},{10,12... | collective-permute-start | bytes 4423688 | tf_op jit(solution)/shard_map/cond/branch_3_fun/ppermute | solution.py:175
  89.6 36.0 %collective-permute-start.35 = (bf16[3,320,768]{2,1,0:T(8,128)(2,1)}, bf16[3,320,768]{2,1,0:T(8,128)(2,1)}, u32[]{:S(2)}, u32[]{:S(2)}) collective-permute-start(bf16[3,320,768]{2,1,0:T(8,128)(2,1)} %param.35), channel_id=1, source_target_pairs={{0,2},{1,3},{2,6},{3,7},{4,4},{5,5},{6,0},{7,1},{8,10},{9,11},{10,... | collective-permute-start | bytes 4423688 | tf_op jit(solution)/shard_map/cond/branch_11_fun/ppermute | solution.py:175
  128.6 1.9 %collective-permute-start.49 = (bf16[320,768]{1,0:T(8,128)(2,1)S(1)}, bf16[320,768]{1,0:T(8,128)(2,1)S(1)}, u32[]{:S(2)}, u32[]{:S(2)}) collective-permute-start(bf16[320,768]{1,0:T(8,128)(2,1)S(1)} %get-tuple-element.142), channel_id=1, source_target_pairs={{0,1},{1,0},{2,3},{3,2},{4,5},{5,4},{6,7},{7,6},{8,9},{9,8},{10,11... | collective-permute-start | bytes 1474568 | tf_op jit(solution)/shard_map/ppermute | solution.py:188
  128.6 10.3 %collective-permute-start.51 = (bf16[320,768]{1,0:T(8,128)(2,1)}, bf16[320,768]{1,0:T(8,128)(2,1)}, u32[]{:S(2)}, u32[]{:S(2)}) collective-permute-start(bf16[320,768]{1,0:T(8,128)(2,1)} %get-tuple-element.145), channel_id=1, source_target_pairs={{0,1},{1,0},{2,3},{3,2},{4,5},{5,4},{6,7},{7,6},{8,9},{9,8},{10,11... | collective-permute-start | bytes 1474568 | tf_op jit(solution)/shard_map/ppermute | solution.py:188
  129.1 12.4 %collective-permute-start.50 = (bf16[320,768]{1,0:T(8,128)(2,1)}, bf16[320,768]{1,0:T(8,128)(2,1)S(1)}, u32[]{:S(2)}, u32[]{:S(2)}) collective-permute-start(bf16[320,768]{1,0:T(8,128)(2,1)} %get-tuple-element.144), channel_id=1, source_target_pairs={{0,1},{1,0},{2,3},{3,2},{4,5},{5,4},{6,7},{7,6},{8,9},{9,8},{10,11... | collective-permute-start | bytes 1474568 | tf_op jit(solution)/shard_map/ppermute | solution.py:188
  133.2 15.3 %all-to-all-start.2 = ((bf16[4,128,768]{1,2,0:T(8,128)(2,1)}), bf16[4,128,768]{1,2,0:T(8,128)(2,1)S(1)}, u32[]{:S(2)}, u32[]{:S(2)}) async-start(bf16[4,128,768]{1,2,0:T(8,128)(2,1)} %fusion.5), calls=%async_computation.2 | async-start | bytes 1572864 | tf_op jit(solution)/shard_map/all_to_all | solution.py:199
